TPU v7x, 32 devices: a whole 2x2x4 slice. The times are simulated.
32 devices in a mesh: dp: 8 (over z, y), mp: 4 (over x, core).
Axes of the slice: x: 2, y: 2, z: 4, core: 2. Of those that a mesh axis runs over, the one named last changes fastest.
Arguments:
- queries: bfloat16 [1024, 8192], P('dp', 'mp'), may hold values from -8 to 8
- tree_keys: bfloat16 [1024, 1024], P('dp', 'mp'), may hold values from -18 to 18
- tree_values: bfloat16 [1024, 1024], P('dp', 'mp'), may hold values from -6 to 6
- cache_keys: bfloat16 [16, 4096, 1024], P('dp', None, 'mp'), may hold values from -8 to 8
- cache_values: bfloat16 [16, 4096, 1024], P('dp', None, 'mp'), may hold values from -6 to 6
- cache_lens: int32 [16], P('dp'), may hold values from 1024 to 4096, as said below
- parents: int32 [16, 64], P('dp'), may hold values from -1 to 62, as said below
- accepted_nodes: int32 [16, 8], P('dp'), may hold values from 0 to 63, as said below
- residual: bfloat16 [1024, 8192], P('dp', 'mp'), may hold values from -1.796875 to 1.796875
- out_weight: bfloat16 [8192, 8192], P('mp', 'dp'), may hold values from -0.0625 to 0.0625
Outputs:
- tree_hidden: bfloat16 [1024, 8192], P('dp', 'mp')
- accepted_hidden: bfloat16 [128, 8192], P(None, 'mp')
Inputs may be any that keep to these rules, and one draw needn't show every extreme that they name: parents[r, 0] = -1 and 0 <= parents[r, i] < i for i >= 1. accepted_nodes[r, 0] = 0, the nodes of a row increase, and parents[r, accepted_nodes[r, a + 1]] = accepted_nodes[r, a]. `cache_lens`: some request has exactly 4096 filled positions.
All inputs are finite; a program needn't handle non-finite values.
Results may differ from a plain program's by a relative error of at most 0.015.
Values may be sent and summed in bfloat16 or wider, within the bound.
A program may use at most 64 MiB of HBM per device.

v0:
```python
import math
import jax
import jax.numpy as jnp
from jax import lax
from jax.sharding import PartitionSpec as P

HEADS = 64
KV_HEADS = 8
HD = 128
neg_large = -1e30


def ancestry(parents, node_count):
    positions = jnp.arange(node_count, dtype=jnp.int32)
    parent_hot = (parents[:, :, None] == positions[None, None, :]).astype(jnp.float32)
    reached = parent_hot + jnp.eye(node_count, dtype=jnp.float32)[None]
    for squaring in range((node_count - 1).bit_length()):
        reached = jnp.minimum(
            jnp.einsum("rij,rjk->rik", reached, reached, precision=lax.Precision.HIGHEST), 1.0
        )
    return reached > 0.5


def per_device(
    queries,
    tree_keys,
    tree_values,
    cache_keys,
    cache_values,
    cache_lens,
    parents,
    accepted_nodes,
    residual,
    out_weight,
):
    request_count = parents.shape[0]
    node_count = parents.shape[1]
    cache_length = cache_keys.shape[1]
    kv_local = tree_keys.shape[1] // HD
    group_size = HEADS // KV_HEADS
    scale_factor = 1.0 / math.sqrt(HD)
    query_grid = queries.reshape(request_count, node_count, kv_local, group_size, HD)
    tree_key_grid = tree_keys.reshape(request_count, node_count, kv_local, HD)
    tree_value_grid = tree_values.reshape(request_count, node_count, kv_local, HD)
    cache_key_grid = cache_keys.reshape(request_count, cache_length, kv_local, HD)
    cache_value_grid = cache_values.reshape(request_count, cache_length, kv_local, HD)
    ancestor = ancestry(parents, node_count)
    tree_scores = (
        jnp.einsum(
            "rnkgd,rjkd->rnkgj", query_grid, tree_key_grid, preferred_element_type=jnp.float32
        )
        * scale_factor
    )
    tree_scores = jnp.where(ancestor[:, :, None, None, :], tree_scores, neg_large)
    run_max = jnp.max(tree_scores, axis=-1)
    tree_weights = jnp.exp(tree_scores - run_max[..., None])
    run_sum = jnp.sum(tree_weights, axis=-1)
    run_acc = jnp.einsum(
        "rnkgj,rjkd->rnkgd",
        tree_weights.astype(jnp.bfloat16),
        tree_value_grid,
        preferred_element_type=jnp.float32,
    )
    block_len = min(512, cache_length)

    def absorb(block_number, state_now):
        old_max, old_sum, old_acc = state_now
        block_start = block_number * block_len
        key_block = lax.dynamic_slice_in_dim(cache_key_grid, block_start, block_len, 1)
        value_block = lax.dynamic_slice_in_dim(cache_value_grid, block_start, block_len, 1)
        block_scores = (
            jnp.einsum(
                "rnkgd,rpkd->rnkgp", query_grid, key_block, preferred_element_type=jnp.float32
            )
            * scale_factor
        )
        positions = block_start + jnp.arange(block_len, dtype=jnp.int32)
        live_keys = positions[None, :] < cache_lens[:, None]
        block_scores = jnp.where(live_keys[:, None, None, None, :], block_scores, neg_large)
        new_max = jnp.maximum(old_max, jnp.max(block_scores, axis=-1))
        block_weights = jnp.exp(block_scores - new_max[..., None])
        rescale = jnp.exp(old_max - new_max)
        new_sum = old_sum * rescale + jnp.sum(block_weights, axis=-1)
        new_acc = old_acc * rescale[..., None] + jnp.einsum(
            "rnkgp,rpkd->rnkgd",
            block_weights.astype(jnp.bfloat16),
            value_block,
            preferred_element_type=jnp.float32,
        )
        return (new_max, new_sum, new_acc)

    trip_count = cache_length // block_len
    run_max, run_sum, run_acc = lax.fori_loop(0, trip_count, absorb, (run_max, run_sum, run_acc))
    attended = (run_acc / run_sum[..., None]).astype(jnp.bfloat16)
    attended = attended.reshape(request_count * node_count, kv_local * group_size * HD)
    feature_share = residual.shape[1]
    all_rows = jnp.dot(
        lax.all_gather(attended, "dp", axis=0, tiled=True),
        out_weight,
        preferred_element_type=jnp.float32,
    )
    partial_sum = lax.all_to_all(
        all_rows.astype(jnp.bfloat16), "dp", split_axis=0, concat_axis=1, tiled=True
    ).astype(all_rows.dtype)
    head_total_sum = lax.psum(partial_sum.astype(jnp.bfloat16), "mp").astype(jnp.float32)
    own_share = lax.dynamic_slice_in_dim(
        head_total_sum, lax.axis_index("mp") * feature_share, feature_share, 1
    )
    tree_hidden = (residual.astype(jnp.float32) + own_share).astype(jnp.bfloat16)
    row_base = jnp.arange(request_count, dtype=jnp.int32)[:, None] * node_count
    picked_rows = (row_base + accepted_nodes).reshape(-1)
    picked_hidden = jnp.take(tree_hidden, picked_rows, axis=0)
    accepted_hidden = lax.all_gather(picked_hidden, "dp", axis=0, tiled=True)
    return (tree_hidden, accepted_hidden)


def solution(mesh):
    placed = (
        P("dp", "mp"),
        P("dp", "mp"),
        P("dp", "mp"),
        P("dp", None, "mp"),
        P("dp", None, "mp"),
        P("dp"),
        P("dp", None),
        P("dp", None),
        P("dp", "mp"),
        P("mp", "dp"),
    )
    return jax.shard_map(
        per_device,
        mesh=mesh,
        in_specs=placed,
        out_specs=(P("dp", "mp"), P(None, "mp")),
        check_vma=False,
    )
```

profile of v0, /device:TPU:0, one launch (start us, length us, event | category | flops | bytes accessed | tf_op | source)
XLA Modules:
  0.0 305.0 jit_solution(8466349382810361783)
XLA Ops:
  7.2 1.1 copy.42
  8.4 1.0 convolution_minimum_fusion.5
  9.8 0.2 convolution_minimum_fusion.2
  10.2 0.2 fusion.26
  10.5 0.9 reshape.112
  11.5 0.6 fusion.38
  12.2 0.3 fusion.27
  12.5 0.3 copy.21
  12.8 0.3 convolution_bitcast_fusion
  13.3 6.4 %copy.23 = bf16[2,4096,256]{1,2,0:T(8,128)(2,1)} copy(bf16[2,4096,256]{2,1,0:T(8,128)(2,1)} %param.15) | data formatting | bytes 8388608 | tf_op args[3]
  19.7 6.4 %copy.24 = bf16[2,4096,256]{1,2,0:T(8,128)(2,1)} copy(bf16[2,4096,256]{2,1,0:T(8,128)(2,1)} %param.16) | data formatting | bytes 8388608 | tf_op args[4]
  26.1 49.3 %while.17 = (s32[]{:T(128)}, f32[2,64,2,8]{1,3,2,0:T(8,128)S(1)}, f32[2,64,2,8]{1,3,2,0:T(8,128)S(1)}, f32[2,64,2,8,128]{4,1,3,2,0:T(8,128)S(1)}, s32[2]{0:T(128...) while((s32[]{:T(128)}, f32[2,64,2,8]{1,3,2,0:T(8,128)S(1)}, ...), condition=%wide.region_5.6_spmd, body=%wide.region_2.5_spmd.sunk | while | flops 548935168 | bytes 16392375 | solution.py:93
  26.2 1.8 bitcast_reduce_fusion.2
  28.0 1.7 fusion.61
  29.7 2.5 fusion.62
  32.3 1.8 bitcast_reduce_fusion.2
  34.2 1.7 fusion.61
  35.9 2.5 fusion.62
  38.5 1.8 bitcast_reduce_fusion.2
  40.3 1.7 fusion.61
  42.1 2.5 fusion.62
  44.7 1.8 bitcast_reduce_fusion.2
  46.5 1.7 fusion.61
  48.2 2.5 fusion.62
  50.8 1.8 bitcast_reduce_fusion.2
  52.7 1.7 fusion.61
  54.4 2.5 fusion.62
  57.0 1.8 bitcast_reduce_fusion.2
  58.9 1.7 fusion.61
  60.6 2.5 fusion.62
  63.2 1.8 bitcast_reduce_fusion.2
  65.0 1.7 fusion.61
  66.7 2.5 fusion.62
  69.3 1.8 bitcast_reduce_fusion.2
  71.2 1.7 fusion.61
  72.9 2.5 fusion.62
  75.4 0.3 divide_convert_fusion
  75.8 0.3 copy.29
  76.1 1.0 reshape.117
  77.2 75.6 %all-gather.2.cloned.1.call-done = bf16[1024,2048]{1,0:T(8,128)(2,1)} async-done(((bf16[128,2048]{1,0:T(8,128)(2,1)}), bf16[1024,2048]{1,0:T(8,128)(2,1)}) %all-gather.2.cloned.1.call-update) | async-done | bytes 4194320 | tf_op jit(solution)/shard_map/all_gather | solution.py:98
  152.8 7.9 %convolution_convert_fusion = bf16[1024,1024]{1,0:T(8,128)(2,1)S(1)} fusion(bf16[1024,2048]{1,0:T(8,128)(2,1)} %all-gather.2.cloned.1.call-done, bf16[2048,1024]{1,0:T(8,128)(2,1)} %param.21), kind=kOutput, calls=%fused_computation.27 | convolution fusion | flops 4296015872 | bytes 10485760 | tf_op jit(solution)/shard_map/dot_general | solution.py:97
  160.8 51.1 %all_to_all.19 = bf16[8,128,1024]{2,1,0:T(8,128)(2,1)S(1)} all-to-all(bf16[8,128,1024]{2,1,0:T(8,128)(2,1)S(1)} %bitcast.87), channel_id=1, replica_groups=mesh['dp'=8,'mp'=4] {'dp'}, dimensions={0} | all-to-all | bytes 4194304 | tf_op jit(solution)/shard_map/all_to_all | solution.py:102
  211.9 1.5 copy.41
  213.7 50.2 %all-reduce.2.cloned.1.call-done = bf16[128,8192]{1,0:T(8,128)(2,1)} async-done(((bf16[128,8192]{1,0:T(8,128)(2,1)}), bf16[128,8192]{1,0:T(8,128)(2,1)}) %all-reduce.2.cloned.1.call-update) | async-done | bytes 2097168 | tf_op jit(solution)/shard_map/psum | solution.py:105
  263.9 1.2 add_convert_fusion
  265.1 0.6 gather_fusion
  265.7 31.6 %all_gather.7 = bf16[128,2048]{1,0:T(8,128)(2,1)S(1)} all-gather(bf16[16,2048]{1,0:T(8,128)(2,1)S(1)} %broadcast_select_fusion), channel_id=1, replica_groups=mesh['dp'=8,'mp'=4] {'dp'}, dimensions={0}, use_global_device_ids=true | all-gather | bytes 589824 | tf_op jit(solution)/shard_map/all_gather | solution.py:113
  297.3 0.8 copy.67
  (70 shorter events, 2.3 us)
Async XLA Ops:
  7.2 5.6 %copy-start.2 = (bf16[128,256]{1,0:T(8,128)(2,1)S(1)}, bf16[128,256]{1,0:T(8,128)(2,1)}, u32[]{:S(2)}) copy-start(bf16[128,256]{1,0:T(8,128)(2,1)} %param.14) | copy-start | bytes 196612
  7.2 145.7 %all-gather.2.cloned.1.call-start = ((), (), s32[]{:S(2)}) async-start(), calls=%async_computation.1 | async-start | bytes 4718592 | tf_op jit(solution)/shard_map/all_gather | solution.py:98
  19.7 6.4 %copy-start.3 = (s32[2]{0:T(128)S(1)}, s32[2]{0:T(128)}, u32[]{:S(2)}) copy-start(s32[2]{0:T(128)} %param.17) | copy-start | bytes 28
  77.2 186.7 %all-reduce.2.cloned.1.call-start = ((), (), s32[]{:S(2)}) async-start(), calls=%async_computation.2 | async-start | bytes 4194304 | tf_op jit(solution)/shard_map/psum | solution.py:105
  211.9 1.5 copy-start.4
  211.9 51.9 %copy-start.1 = (bf16[128,2048]{1,0:T(8,128)(2,1)S(1)}, bf16[128,2048]{1,0:T(8,128)(2,1)}, u32[]{:S(2)}) copy-start(bf16[128,2048]{1,0:T(8,128)(2,1)} %param.20) | copy-start | bytes 1572868
  265.1 33.1 %copy-start = (bf16[128,2048]{1,0:T(8,128)(2,1)}, bf16[128,2048]{1,0:T(8,128)(2,1)S(1)}, u32[]{:S(2)}) copy-start(bf16[128,2048]{1,0:T(8,128)(2,1)S(1)} %add_convert_fusion) | copy-start | bytes 1572868
Sparse Core Ops, SparseCore 0:
  77.3 75.5 all-gather.1
  213.5 50.2 all-reduce.1
where the time goes:
time: 306 us; the launch traced here: 305 us
  waiting for transfers between devices  126 us (41%)
  blocking collectives  82.7 us (27%)
  matrix products  45.3 us (15%)
  local copies, waits for them, and re-layouts  20 us (7%)
  other arithmetic  16.3 us (5%)
  between operations  14.2 us (5%)
    all_gather x1, waiting for transfers between devices, per_device(): lax.all_gather(attended, 'dp', axis=0, tiled=True)  75.6 us
    all_to_all x1, blocking collectives, per_device(): lax.all_to_all(all_rows.astype(jnp.bfloat16), 'dp', split_axis=0, concat_...  51.1 us
    psum x1, waiting for transfers between devices, per_device(): lax.psum(partial_sum.astype(jnp.bfloat16), 'mp').astype(jnp.float32)  50.2 us
    all_gather x1, blocking collectives, per_device(): accepted_hidden = lax.all_gather(picked_hidden, 'dp', axis=0, tiled=True)  31.6 us
    dot_general x8, matrix products, absorb(): jnp.einsum('rnkgp,rpkd->rnkgd', block_weights.astype(jnp.bfloat16), value...  19.8 us
    unnamed x14, local copies, waits for them, and re-layouts  14.7 us
    dot_general x8, matrix products, absorb(): jnp.einsum('rnkgd,rpkd->rnkgp', query_grid, key_block, preferred_element_...  14.7 us
    reduce_sum x8, other arithmetic, absorb(): new_sum = old_sum * rescale + jnp.sum(block_weights, axis=-1)  13.6 us
  transfers between devices with their start and end apart: 2, of which 2 were waited for; matrix products, arithmetic and copies ran while one was open for 0% of the time, Pallas kernels for 0%

commit v1 on v0

--- a/solution.py
+++ b/solution.py
@@ -99,8 +99,14 @@
         out_weight,
         preferred_element_type=jnp.float32,
     )
-    partial_sum = lax.all_to_all(
-        all_rows.astype(jnp.bfloat16), "dp", split_axis=0, concat_axis=1, tiled=True
+    partial_sum = jnp.concatenate(
+        lax.all_to_all(
+            jnp.stack(jnp.split(all_rows.astype(jnp.bfloat16), lax.axis_size("dp"), axis=0)),
+            "dp",
+            0,
+            0,
+        ),
+        axis=1,
     ).astype(all_rows.dtype)
     head_total_sum = lax.psum(partial_sum.astype(jnp.bfloat16), "mp").astype(jnp.float32)
     own_share = lax.dynamic_slice_in_dim(

time: 306 us -> 311 us (1.016)
  local copies, waits for them, and re-layouts: 20 us -> 25.2 us
    reshape x0 -> x2, local copies, waits for them, and re-layouts: none -> 6.53 us  [per_device(): jnp.concatenate(lax.all_to_all(jnp.stack(jnp.split(all_rows.astype(jnp.bf...]
    unnamed x14 -> x23, local copies, waits for them, and re-layouts: 14.7 us -> 15.7 us
where the time goes in v1:
time: 311 us; the launch traced here: 310 us
  waiting for transfers between devices  125 us (40%)
  blocking collectives  82.7 us (27%)
  matrix products  45.3 us (15%)
  local copies, waits for them, and re-layouts  25.2 us (8%)
  other arithmetic  16.3 us (5%)
  between operations  14.3 us (5%)
    all_gather x1, waiting for transfers between devices, per_device(): lax.all_gather(attended, 'dp', axis=0, tiled=True)  75.6 us
    all_to_all x1, blocking collectives, per_device(): lax.all_to_all(jnp.stack(jnp.split(all_rows.astype(jnp.bfloat16), lax.axi...  51.1 us
    psum x1, waiting for transfers between devices, per_device(): lax.psum(partial_sum.astype(jnp.bfloat16), 'mp').astype(jnp.float32)  49.5 us
    all_gather x1, blocking collectives, per_device(): accepted_hidden = lax.all_gather(picked_hidden, 'dp', axis=0, tiled=True)  31.6 us
    dot_general x8, matrix products, absorb(): jnp.einsum('rnkgp,rpkd->rnkgd', block_weights.astype(jnp.bfloat16), value...  19.8 us
    unnamed x23, local copies, waits for them, and re-layouts  15.7 us
    dot_general x8, matrix products, absorb(): jnp.einsum('rnkgd,rpkd->rnkgp', query_grid, key_block, preferred_element_...  14.7 us
    reduce_sum x8, other arithmetic, absorb(): new_sum = old_sum * rescale + jnp.sum(block_weights, axis=-1)  13.6 us
  transfers between devices with their start and end apart: 2, of which 2 were waited for; matrix products, arithmetic and copies ran while one was open for 0% of the time, Pallas kernels for 0%

profile of v1, /device:TPU:0, one launch (start us, length us, event | category | flops | bytes accessed | tf_op | source)
XLA Modules:
  0.0 309.6 jit_solution(12215268202503081583)
XLA Ops:
  7.2 1.1 copy.41
  8.4 1.0 convolution_minimum_fusion.5
  10.2 0.2 fusion.26
  10.7 0.6 fusion.46
  11.4 0.3 fusion.27
  11.6 0.3 copy.20
  12.0 0.3 convolution_bitcast_fusion
  12.5 6.4 %copy.22 = bf16[2,4096,256]{1,2,0:T(8,128)(2,1)} copy(bf16[2,4096,256]{2,1,0:T(8,128)(2,1)} %param.15) | data formatting | bytes 8388608 | tf_op args[3]
  18.9 6.5 %copy.23 = bf16[2,4096,256]{1,2,0:T(8,128)(2,1)} copy(bf16[2,4096,256]{2,1,0:T(8,128)(2,1)} %param.16) | data formatting | bytes 8388608 | tf_op args[4]
  25.4 49.3 %while.17 = (s32[]{:T(128)}, f32[2,64,2,8]{1,3,2,0:T(8,128)S(1)}, f32[2,64,2,8]{1,3,2,0:T(8,128)S(1)}, f32[2,64,2,8,128]{4,1,3,2,0:T(8,128)S(1)}, s32[2]{0:T(128...) while((s32[]{:T(128)}, f32[2,64,2,8]{1,3,2,0:T(8,128)S(1)}, ...), condition=%wide.region_5.6_spmd, body=%wide.region_2.5_spmd.sunk | while | flops 548935168 | bytes 16392375 | solution.py:93
  25.5 1.8 bitcast_reduce_fusion.2
  27.4 1.7 fusion.69
  29.1 2.5 fusion.70
  31.7 1.8 bitcast_reduce_fusion.2
  33.5 1.7 fusion.69
  35.3 2.5 fusion.70
  37.8 1.8 bitcast_reduce_fusion.2
  39.7 1.7 fusion.69
  41.4 2.5 fusion.70
  44.0 1.8 bitcast_reduce_fusion.2
  45.9 1.7 fusion.69
  47.6 2.5 fusion.70
  50.2 1.8 bitcast_reduce_fusion.2
  52.0 1.7 fusion.69
  53.8 2.5 fusion.70
  56.4 1.8 bitcast_reduce_fusion.2
  58.2 1.7 fusion.69
  59.9 2.5 fusion.70
  62.5 1.8 bitcast_reduce_fusion.2
  64.4 1.7 fusion.69
  66.1 2.5 fusion.70
  68.7 1.8 bitcast_reduce_fusion.2
  70.5 1.7 fusion.69
  72.3 2.5 fusion.70
  74.8 0.3 divide_convert_fusion
  75.1 0.3 copy.28
  75.5 1.0 reshape.120
  76.6 75.6 %all-gather.2.cloned.1.call-done = bf16[1024,2048]{1,0:T(8,128)(2,1)} async-done(((bf16[128,2048]{1,0:T(8,128)(2,1)}), bf16[1024,2048]{1,0:T(8,128)(2,1)}) %all-gather.2.cloned.1.call-update) | async-done | bytes 4194320 | tf_op jit(solution)/shard_map/all_gather | solution.py:98
  152.2 7.9 %convolution_convert_fusion = bf16[1024,1024]{1,0:T(8,128)(2,1)S(1)} fusion(bf16[1024,2048]{1,0:T(8,128)(2,1)} %all-gather.2.cloned.1.call-done, bf16[2048,1024]{1,0:T(8,128)(2,1)} %param.21), kind=kOutput, calls=%fused_computation.27 | convolution fusion | flops 4296015872 | bytes 10485760 | tf_op jit(solution)/shard_map/dot_general | solution.py:97
  160.3 51.1 %all_to_all.5 = bf16[8,128,1024]{2,1,0:T(8,128)(2,1)S(1)} all-to-all(bf16[8,128,1024]{2,1,0:T(8,128)(2,1)S(1)} %fusion.29), channel_id=1, replica_groups=mesh['dp'=8,'mp'=4] {'dp'}, dimensions={0} | all-to-all | bytes 4194304 | tf_op jit(solution)/shard_map/all_to_all | solution.py:103
  211.5 2.4 copy.29
  213.9 4.1 %copy.30 = bf16[128,8192]{1,0:T(8,128)(2,1)} copy(bf16[128,8192]{0,1:T(8,128)(2,1)} %bitcast.113) | data formatting | bytes 4194304 | tf_op jit(solution)/shard_map/reshape | solution.py:102
  218.1 0.6 copy-done.5
  219.0 49.5 %all-reduce.2.cloned.1.call-done = bf16[128,8192]{1,0:T(8,128)(2,1)} async-done(((bf16[128,8192]{1,0:T(8,128)(2,1)}), bf16[128,8192]{1,0:T(8,128)(2,1)}) %all-reduce.2.cloned.1.call-update) | async-done | bytes 2097168 | tf_op jit(solution)/shard_map/psum | solution.py:111
  268.5 1.2 add_convert_fusion
  269.7 0.6 gather_fusion
  270.4 31.6 %all_gather.7 = bf16[128,2048]{1,0:T(8,128)(2,1)S(1)} all-gather(bf16[16,2048]{1,0:T(8,128)(2,1)S(1)} %broadcast_select_fusion), channel_id=1, replica_groups=mesh['dp'=8,'mp'=4] {'dp'}, dimensions={0}, use_global_device_ids=true | all-gather | bytes 589824 | tf_op jit(solution)/shard_map/all_gather | solution.py:119
  301.9 0.8 copy.73
  (81 shorter events, 2.7 us)
Async XLA Ops:
  7.2 3.4 %copy-start.2 = (bf16[128,256]{1,0:T(8,128)(2,1)S(1)}, bf16[128,256]{1,0:T(8,128)(2,1)}, u32[]{:S(2)}) copy-start(bf16[128,256]{1,0:T(8,128)(2,1)} %param.13) | copy-start | bytes 196612
  7.2 145.0 %all-gather.2.cloned.1.call-start = ((), (), s32[]{:S(2)}) async-start(), calls=%async_computation.1 | async-start | bytes 4718592 | tf_op jit(solution)/shard_map/all_gather | solution.py:98
  10.7 1.3 copy-start.3
  18.9 6.5 %copy-start.4 = (s32[2]{0:T(128)S(1)}, s32[2]{0:T(128)}, u32[]{:S(2)}) copy-start(s32[2]{0:T(128)} %param.17) | copy-start | bytes 28
  76.5 192.0 %all-reduce.2.cloned.1.call-start = ((), (), s32[]{:S(2)}) async-start(), calls=%async_computation.2 | async-start | bytes 4194304 | tf_op jit(solution)/shard_map/psum | solution.py:111
  218.0 0.7 copy-start.5
  218.0 50.5 %copy-start.1 = (bf16[128,2048]{1,0:T(8,128)(2,1)S(1)}, bf16[128,2048]{1,0:T(8,128)(2,1)}, u32[]{:S(2)}) copy-start(bf16[128,2048]{1,0:T(8,128)(2,1)} %param.20) | copy-start | bytes 1572868
  269.7 33.1 %copy-start = (bf16[128,2048]{1,0:T(8,128)(2,1)}, bf16[128,2048]{1,0:T(8,128)(2,1)S(1)}, u32[]{:S(2)}) copy-start(bf16[128,2048]{1,0:T(8,128)(2,1)S(1)} %add_convert_fusion) | copy-start | bytes 1572868
Sparse Core Ops, SparseCore 0:
  76.6 75.5 all-gather.1
  218.2 50.2 all-reduce.1
